TPU v7x, 256 devices: a whole 4x4x8 slice. The times are simulated.
256 devices in a mesh: gx: 4 (over x), gy: 8 (over z_hi, y), gz: 8 (over z_lo, core).
Axes of the slice: x: 4, y: 4, z: 8 (z_hi: 2, z_lo: 4; z = z_hi * 4 + z_lo), core: 2. Of those that a mesh axis runs over, the one named last changes fastest.
Arguments:
- velocity: float32 [3, 128, 768, 2048], P(None, 'gx', 'gy', 'gz'), may hold values from -6 to 6
Outputs:
- magnitude: float32 [128, 768, 2048], P('gx', ('gy', 'gz'))
- level_one: float32 [64, 384, 1024], P('gx', 'gy')
- level_two: float32 [32, 192, 512], P('gx', 'gy')
- level_three: float32 [16, 96, 256], P('gx', 'gy')
- level_four: float32 [8, 48, 128], P('gx', 'gy')
- level_five: float32 [4, 24, 64], P('gx', 'gy')
All inputs are finite; a program needn't handle non-finite values.
Results may differ from a plain program's by a relative error of at most 0.000075.
Values sent between devices are 32-bit elements; how exact they have to be, the bound alone decides.
No kernel may reach another device: no remote copies, remote signals or barrier semaphores. Data moves between devices by JAX's collectives and lax.ppermute only.
A program may use at most 256 MiB of HBM per device.

v0:
```python
import functools

import jax
import jax.numpy as jnp
from jax import lax
from jax.experimental import pallas as pl
from jax.experimental.pallas import tpu as pltpu
from jax.sharding import PartitionSpec as P


PLANES = 8
HIGHEST = lax.Precision.HIGHEST
F32 = jnp.float32


def pairing(depth):
    row = lax.broadcasted_iota(jnp.int32, (depth, depth // 2), 0)
    col = lax.broadcasted_iota(jnp.int32, (depth, depth // 2), 1)
    return (lax.div(row, jnp.int32(2)) == col).astype(F32)


def pair_lanes(value):
    _, depth = value.shape
    width = min(depth, 256)
    matrix = pairing(width)
    parts = [
        jnp.dot(value[:, i : i + width], matrix, precision=HIGHEST, preferred_element_type=F32)
        for i in range(0, depth, width)
    ]
    return parts[0] if len(parts) == 1 else jnp.concatenate(parts, axis=1)


def keep_rows(scratch, at, value):
    for t in range(scratch.shape[0]):
        scratch[t, at : at + value.shape[0], :] = value[:, t * 128 : (t + 1) * 128]


def pair_rows(scratch, pairs):
    parts = [
        scratch[t, pl.ds(0, pairs, stride=2), :] + scratch[t, pl.ds(1, pairs, stride=2), :]
        for t in range(scratch.shape[0])
    ]
    return parts[0] if len(parts) == 1 else jnp.concatenate(parts, axis=1)


def lanes_at(k, x):
    last = 2 * (k * 32 + x)
    return last, lax.rem(last + 127, 128)


def ends_kernel(
    velocity, x_first, x_last, y_first, y_last, z_first, z_last, uv, w_planes, w_rows, sems
):
    _, X, rows, depth = velocity.shape
    chunk = 4
    chunks = X // chunk
    pieces = [
        (velocity.at[0:2, c * chunk : (c + 1) * chunk], uv.at[:, c * chunk : (c + 1) * chunk])
        for c in range(chunks)
    ]
    pieces += [(velocity.at[2, at], w_planes.at[i]) for i, at in enumerate((0, X - 1))]
    pieces += [
        (velocity.at[2, :, at : at + 8, :], w_rows.at[i]) for i, at in enumerate((0, rows - 8))
    ]
    copies = [pltpu.make_async_copy(a, b, sems.at[i]) for i, (a, b) in enumerate(pieces)]
    for copy in copies:
        copy.start()
    lane = lax.broadcasted_iota(jnp.int32, (rows, 128), 1)
    first = jnp.zeros((rows, 128), F32)
    last = jnp.zeros((rows, 128), F32)
    for c in range(chunks):
        copies[c].wait()
        for p in range(c * chunk, (c + 1) * chunk):
            for k in range(2):
                to_last = 2 * (k * 32 + p)
                to_first = (to_last + 127) % 128
                first = jnp.where(
                    lane == to_first, pltpu.roll(uv[k, p, :, :128], to_first, 1), first
                )
                last = jnp.where(
                    lane == to_last,
                    pltpu.roll(uv[k, p, :, depth - 128 :], (to_last + 1) % 128, 1),
                    last,
                )
            y_first[0, p : p + 1, :] = uv[0, p, 0:1, :]
            y_last[0, p : p + 1, :] = uv[0, p, rows - 1 : rows, :]
    z_first[...] = first
    z_last[...] = last
    for copy in copies[chunks:]:
        copy.wait()
    for i, (out, at) in enumerate(((x_first, 0), (x_last, X - 1))):
        out[0] = uv[1, at]
        out[1] = w_planes[i]
    for p in range(X):
        y_first[1, p : p + 1, :] = w_rows[0, p, 0:1, :]
        y_last[1, p : p + 1, :] = w_rows[1, p, 7:8, :]


def ends(velocity):
    _, X, Y, Z = velocity.shape
    outs = [jax.ShapeDtypeStruct(s, F32) for s in ((2, Y, Z), (2, X, Z), (Y, 128)) for _ in range(2)]
    return pl.pallas_call(
        ends_kernel,
        in_specs=[pl.BlockSpec(memory_space=pl.ANY)],
        out_specs=[pl.BlockSpec(memory_space=pltpu.VMEM)] * 6,
        out_shape=outs,
        scratch_shapes=[
            pltpu.VMEM((2, X, Y, Z), F32),
            pltpu.VMEM((2, Y, Z), F32),
            pltpu.VMEM((2, X, 8, Z), F32),
            pltpu.SemaphoreType.DMA((X // 4 + 4,)),
        ],
        compiler_params=pltpu.CompilerParams(vmem_limit_bytes=53 << 20),
        cost_estimate=pl.CostEstimate(flops=4_000_000, bytes_accessed=8_000_000, transcendentals=0),
        name="ends",
    )(velocity)


def curl_kernel(shifts, each, with_level, which, bands, pos, vel, v_before, v_after, w_before, w_after, *refs):
    if bands > 1:
        above, below = refs[:2]
        refs = refs[2:]
    x_before, x_after, y_before, y_after, z_before, z_after = refs[:6]
    count = len(shifts)
    if with_level:
        level_out, turned, summed = refs[-3:]
        mags = refs[-3 - count : -3]
    else:
        turned = refs[-1]
        mags = refs[-1 - count : -1]
    band_at, me = pos[which], pos[0]
    step = pl.program_id(0)
    _, planes, rows, depth = vel.shape
    tall = 2 * each
    tiles = depth // 128
    lane = lax.broadcasted_iota(jnp.int32, (tall, 128), 1)
    at_first, at_last, even_lane = lane == 0, lane == 127, lane % 2 == 0
    at_top, at_bottom = band_at == 0, band_at == bands - 1
    at_start = step == 0
    row0 = pl.multiple_of(band_at * rows, 8)
    at_end = step == pl.num_programs(0) - 1

    for pair in range(planes // 2):
        for q in range(rows // tall):
            lo, hi = q * tall, (q + 1) * tall
            band = slice(lo, hi)
            both = []
            here = pl.ds(row0 + lo, tall)
            fills = jnp.where(even_lane, z_before[here, :], z_after[here, :])
            for p in (2 * pair, 2 * pair + 1):

                def first_diff(k):
                    if p + 1 < planes:
                        ahead = vel[k, p + 1, band, :]
                    else:
                        near = (v_after, w_after)[k - 1][0, 0, band, :]
                        ahead = jnp.where(at_end, x_after[k - 1, here, :], near)
                    if p > 0:
                        behind = vel[k, p - 1, band, :]
                    else:
                        near = (v_before, w_before)[k - 1][0, 0, band, :]
                        behind = jnp.where(at_start, x_before[k - 1, here, :], near)
                    return ahead - behind

                def second_diff(k):
                    slot = 0 if k == 0 else 1
                    if lo == 0:
                        edge = y_before[slot, pl.ds(step * planes + p, 1), :]
                        if bands > 1:
                            edge = jnp.where(at_top, edge, above[k, p, 7:8, :])
                        behind = jnp.concatenate([edge, vel[k, p, 0 : hi - 1, :]], axis=0)
                    else:
                        behind = vel[k, p, lo - 1 : hi - 1, :]
                    if hi == rows:
                        edge = y_after[slot, pl.ds(step * planes + p, 1), :]
                        if bands > 1:
                            edge = jnp.where(at_bottom, edge, below[k, p, 0:1, :])
                        ahead = jnp.concatenate([vel[k, p, lo + 1 : hi, :], edge], axis=0)
                    else:
                        ahead = vel[k, p, lo + 1 : hi + 1, :]
                    return ahead - behind

                def third_diff(k):
                    last, _ = lanes_at(k, step * planes + p)
                    fill = pltpu.roll(fills, lax.rem(128 - last, 128), 1)
                    parts = [vel[k, p, band, t * 128 : (t + 1) * 128] for t in range(tiles)]
                    on = [pltpu.roll(part, 127, 1) for part in parts] + [fill]
                    back = [fill] + [pltpu.roll(part, 1, 1) for part in parts]
                    return jnp.concatenate(
                        [
                            jnp.where(at_last, on[t + 1], on[t])
                            - jnp.where(at_first, back[t], back[t + 1])
                            for t in range(tiles)
                        ],
                        axis=1,
                    )

                one = second_diff(2) - third_diff(1)
                two = third_diff(0) - first_diff(2)
                three = first_diff(1) - second_diff(0)
                square = 1.0 + 0.25 * (one * one + two * two + three * three)
                mag = square * lax.rsqrt(square)
                both.append(mag)
                for t in range(tiles):
                    turned[t, pl.ds(lo * planes + p, tall, stride=planes), :] = mag[
                        :, t * 128 : (t + 1) * 128
                    ]
            if with_level:
                keep_rows(summed, pair * rows + lo, both[0] + both[1])
    if with_level:
        level = pair_lanes(pair_rows(summed, planes // 2 * rows // 2)) * 0.125
        level_out[...] = level.reshape(planes // 2, rows // 2, depth // 2)
    size = each * planes
    mask = rows // each - 1
    for m, out in zip(shifts, mags):
        at = pl.multiple_of(size * jnp.bitwise_and(jnp.bitwise_xor(me, m), mask), size)
        for t in range(tiles):
            for y in range(each):
                out[y, :, t * 128 : (t + 1) * 128] = turned[t, pl.ds(at + y * planes, planes), :]


def curl(velocity, shifts, pos, which, bands, halos, with_level=True, n=8):
    _, X, Y, Z = velocity.shape
    H = Y // bands
    each = Y // n
    planes = PLANES
    tiles = Z // 128
    (x_before, x_after), (y_before, y_after), (z_before, z_after) = halos

    def single(comp, shift):
        def index(i, pos):
            at = jnp.minimum(jnp.maximum(i * planes + shift, 0), X - 1)
            return (comp, at, pos[which], 0)

        return pl.BlockSpec((1, 1, H, Z), index)

    def beside(shift):
        def index(i, pos):
            at = pos[which] * (H // 8) + shift
            return (0, i, jnp.minimum(jnp.maximum(at, 0), Y // 8 - 1), 0)

        return pl.BlockSpec((3, planes, 8, Z), index)

    in_specs = [
        pl.BlockSpec((3, planes, H, Z), lambda i, pos: (0, i, pos[which], 0)),
        single(1, -1),
        single(1, planes),
        single(2, -1),
        single(2, planes),
        *([beside(-1), beside(H // 8)] if bands > 1 else []),
        *[pl.BlockSpec(memory_space=pltpu.VMEM)] * 6,
    ]
    args = [velocity] * (7 if bands > 1 else 5) + [x_before, x_after, y_before, y_after, z_before, z_after]
    out_specs = [pl.BlockSpec((each, planes, Z), lambda i, pos: (0, i, 0))] * len(shifts)
    out_shape = [jax.ShapeDtypeStruct((each, X, Z), F32)] * len(shifts)
    scratch = [pltpu.VMEM((tiles, planes * H, 128), F32)]
    if with_level:
        out_specs.append(pl.BlockSpec((planes // 2, H // 2, Z // 2), lambda i, pos: (i, pos[which], 0)))
        out_shape.append(jax.ShapeDtypeStruct((X // 2, Y // 2, Z // 2), F32))
        scratch.append(pltpu.VMEM((tiles, planes // 2 * H, 128), F32))
    cells = X * H * Z
    return pl.pallas_call(
        functools.partial(curl_kernel, shifts, each, with_level, which, bands),
        grid_spec=pltpu.PrefetchScalarGridSpec(
            num_scalar_prefetch=1,
            grid=(X // planes,),
            in_specs=in_specs,
            out_specs=out_specs,
            scratch_shapes=scratch,
        ),
        out_shape=out_shape,
        compiler_params=pltpu.CompilerParams(vmem_limit_bytes=50 << 20),
        cost_estimate=pl.CostEstimate(
            flops=20 * cells, bytes_accessed=20 * cells, transcendentals=cells
        ),
        name="curl",
    )(pos, *args)


def lay_kernel(shifts, pos, *refs):
    blocks = refs[: len(shifts)]
    out, away = refs[-2:]
    depth = blocks[0].shape[2]
    copies = []
    for k, (m, block) in enumerate(zip(shifts, blocks)):
        at = pl.multiple_of(jnp.bitwise_xor(pos[0], m) * depth, depth)
        copies.append(pltpu.make_async_copy(block, out.at[:, :, pl.ds(at, depth)], away.at[k]))
    for copy in copies:
        copy.start()
    for copy in copies:
        copy.wait()


def lay(blocks, shifts, pos, pencil=None, n=8):
    each, X, Z = blocks[0].shape
    count = len(shifts)
    anywhere = pl.BlockSpec(memory_space=pl.ANY)
    in_specs = [pl.BlockSpec(memory_space=pltpu.SMEM)] + [anywhere] * count
    args = [pos, *blocks]
    aliases = {}
    if pencil is not None:
        in_specs.append(anywhere)
        args.append(pencil)
        aliases = {count + 1: 0}
    return pl.pallas_call(
        functools.partial(lay_kernel, shifts),
        in_specs=in_specs,
        out_specs=anywhere,
        out_shape=jax.ShapeDtypeStruct((each, X, n * Z), F32),
        scratch_shapes=[pltpu.SemaphoreType.DMA((count,))],
        compiler_params=pltpu.CompilerParams(vmem_limit_bytes=1 << 20),
        input_output_aliases=aliases,
        cost_estimate=pl.CostEstimate(
            flops=count * each * X * Z, bytes_accessed=8 * count * each * X * Z, transcendentals=0
        ),
        name="lay",
    )(*args)


def levels_kernel(pos, *refs):
    blocks = refs[:8]
    one, two, three, four, five, s1, s2, s3, s4 = refs[8:]
    width = blocks[0].shape[2]
    me = pos[0]
    near = jnp.where(me < 4, 4, 2) + jnp.bitwise_and(me, 1)
    far = jnp.where(me < 4, 6, 0) + jnp.bitwise_and(me, 1)
    sources = (me, jnp.bitwise_xor(me, 2), near, far)
    for k, block in enumerate(blocks):
        source = jnp.bitwise_xor(sources[k % 4], k // 4)
        at = pl.multiple_of(source * width, width)
        one[:, :, pl.ds(at, width)] = block[...]

    def up(planes, scratch):
        half, count = len(planes) // 2, planes[0].shape[0]
        for i in range(half):
            keep_rows(scratch, i * count, planes[2 * i] + planes[2 * i + 1])
        result = pair_lanes(pair_rows(scratch, half * count // 2)) * 0.125
        return [result[i * (count // 2) : (i + 1) * (count // 2), :] for i in range(half)]

    planes = up([one[i] for i in range(one.shape[0])], s1)
    for i, plane in enumerate(planes):
        two[i] = plane
    for target, scratch in ((three, s2), (four, s3), (five, s4)):
        planes = up(planes, scratch)
        for i, plane in enumerate(planes):
            for j in range(plane.shape[0]):
                target[j, i : i + 1, :] = plane[j : j + 1, :]


def levels(blocks, pos, n=8):
    planes, rows, width = blocks[0].shape
    depth = width * n
    shapes = [(planes >> k, rows >> k, depth >> k) for k in range(5)]
    outs = shapes[:2] + [(r, p, d) for p, r, d in shapes[2:]]
    vmem = pl.BlockSpec(memory_space=pltpu.VMEM)
    return pl.pallas_call(
        levels_kernel,
        in_specs=[pl.BlockSpec(memory_space=pltpu.SMEM)] + [vmem] * len(blocks),
        out_specs=[vmem] * 5,
        out_shape=[jax.ShapeDtypeStruct(s, F32) for s in outs],
        scratch_shapes=[pltpu.VMEM((s[2] // 128, s[0] // 2 * s[1], 128), F32) for s in shapes[:4]],
        cost_estimate=pl.CostEstimate(
            flops=4 * planes * rows * depth, bytes_accessed=10 * planes * rows * depth, transcendentals=0
        ),
        compiler_params=pltpu.CompilerParams(vmem_limit_bytes=24 << 20),
        name="levels",
    )(pos, *blocks)


def send(value, pairs):
    return lax.ppermute(value, "gz", pairs)


def swap(value, m):
    return send(value, [(i, i ^ m) for i in range(lax.axis_size("gz"))])


def chips(value, pairs):
    return send(value, [(2 * a + core, 2 * b + core) for a, b in pairs for core in (0, 1)])


def exchange(first, last, axis):
    peers = lax.axis_size(axis)
    up = [(i, (i + 1) % peers) for i in range(peers)]
    down = [(j, i) for i, j in up]
    return lax.ppermute(last, axis, up), lax.ppermute(first, axis, down)


def on_device(velocity):
    at = lax.axis_index("gz").astype(jnp.int32)
    pos = jnp.stack([at, lax.shift_right_logical(at, jnp.int32(1)) ^ 2, jnp.int32(0)])
    x_first, x_last, y_first, y_last, z_first, z_last = ends(velocity)
    y_halo = exchange(y_first, y_last, "gy")
    x_halo = exchange(x_first, x_last, "gx")
    z_halo = exchange(z_first, z_last, "gz")
    halos = (x_halo, y_halo, z_halo)
    blocks = {}
    blocks[4], blocks[5] = curl(velocity, (4, 5), pos, 1, 4, halos, with_level=False)
    *rest, level = curl(velocity, (0, 1, 2, 3, 6, 7), pos, 2, 1, halos)
    blocks.update(zip((0, 1, 2, 3, 6, 7), rest))
    side = swap(level, 2)
    across = [(1, 2), (2, 1)]
    outward = [(1, 0), (2, 3)]
    close = chips(level, across)
    distant = chips(level, [(0, 2), (3, 1)])
    close_out = chips(close, outward)
    distant_out = chips(distant, outward)
    mine = [level, side, close + close_out, distant + distant_out]
    theirs = [swap(value, 1) for value in mine]
    got = {0: blocks[0]}
    for m in range(1, 8):
        got[m] = swap(blocks[m], m)
    upper = levels([*mine, *theirs], pos)
    upper = [*upper[:2]] + [jnp.transpose(value, (1, 0, 2)) for value in upper[2:]]
    pencil = None
    for which in LAYS:
        pencil = lay([got[m] for m in which], which, pos, pencil)
    return (jnp.transpose(pencil, (1, 0, 2)), *upper)


LAYS = ((0, 1, 3, 4, 5), (2, 6, 7))


def solution(mesh):
    in_specs = (P(None, "gx", "gy", "gz"),)
    out_specs = (
        P("gx", ("gy", "gz"), None),
        P("gx", "gy", None),
        P("gx", "gy", None),
        P("gx", "gy", None),
        P("gx", "gy", None),
        P("gx", "gy", None),
    )

    return jax.shard_map(
        on_device, mesh=mesh, in_specs=in_specs, out_specs=out_specs, check_vma=False
    )
```

profile of v0, /device:TPU:25, one launch (start us, length us, event | category | flops | bytes accessed | tf_op | source)
XLA Modules:
  0.0 134.1 jit_solution(12995559768730094620)
XLA Ops:
  0.6 3.5 %ends.1 = (f32[2,96,256]{2,1,0:T(8,128)S(1)}, f32[2,96,256]{2,1,0:T(8,128)S(1)}, f32[2,32,256]{2,1,0:T(8,128)S(1)}, f32[2,32,256]{2,1,0:T(8,128)S(1)}, f32[96,128]{1,0:T(8,128)S(1)}, /*index=5*/f32[96,128]{1,0:T(8,128)S(1)}) custom-call(f32[3,32,96,256]{3,2,1,0:T(8,128)} %refs_1_.1), custom_call_target="tpu_custom_call" | custom-call | flops 4000000 | bytes 8000000 | tf_op jit(solution)/shard_map/ends/pallas_call | solution.py:102
  4.1 1.3 collective-permute-start
  5.4 1.5 %collective-permute-start.1 = (f32[2,96,256]{2,1,0:T(8,128)S(1)}, f32[2,96,256]{2,1,0:T(8,128)S(1)}, u32[]{:S(2)}, u32[]{:S(2)}) collective-permute-start(f32[2,96,256]{2,1,0:T(8,128)S(1)} %get-tuple-element.27), channel_id=1, source_target_pairs={{64,0},{128,64},{192,128},{0,192},{65,1},{129,65},{193,129},{1,193... | collective-permute-start | bytes 589832 | tf_op jit(solution)/shard_map/ppermute | solution.py:386
  6.9 2.8 %collective-permute-start.4 = (f32[96,128]{1,0:T(8,128)S(1)}, f32[96,128]{1,0:T(8,128)S(1)}, u32[]{:S(2)}, u32[]{:S(2)}) collective-permute-start(f32[96,128]{1,0:T(8,128)S(1)} %get-tuple-element.30), channel_id=1, source_target_pairs={{0,1},{1,2},{2,3},{3,4},{4,5},{5,6},{6,7},{7,0},{8,9},{9,10},{10,1... | collective-permute-start | bytes 147464 | tf_op jit(solution)/shard_map/ppermute | solution.py:386
  9.7 5.7 %collective-permute-start.2 = (f32[2,32,256]{2,1,0:T(8,128)S(1)}, f32[2,32,256]{2,1,0:T(8,128)S(1)}, u32[]{:S(2)}, u32[]{:S(2)}) collective-permute-start(f32[2,32,256]{2,1,0:T(8,128)S(1)} %get-tuple-element.28), channel_id=1, source_target_pairs={{0,8},{8,16},{16,24},{24,32},{32,40},{40,48},{48,56},{56,0},{1,9},... | collective-permute-start | bytes 196616 | tf_op jit(solution)/shard_map/ppermute | solution.py:386
  15.3 0.0 collective-permute-start.3
  15.3 0.0 collective-permute-done.4.refs_4_.refs_6_
  15.3 0.0 collective-permute-start.5
  15.3 0.1 pad_add_fusion.pos
  15.4 4.8 %collective-permute-done.5.refs_5_.refs_7_ = f32[96,128]{1,0:T(8,128)S(1)} collective-permute-done((f32[96,128]{1,0:T(8,128)S(1)}, f32[96,128]{1,0:T(8,128)S(1)}, u32[]{:S(2)}, u32[]{:S(2)}) %collective-permute-start.5) | collective-permute-done | bytes 49184 | tf_op jit(solution)/shard_map/ppermute | solution.py:386
  20.2 0.0 collective-permute-done.2.refs_2_.refs_4_
  20.2 5.3 %collective-permute-done.3.refs_3_.refs_5_ = f32[2,32,256]{2,1,0:T(8,128)S(1)} collective-permute-done((f32[2,32,256]{2,1,0:T(8,128)S(1)}, f32[2,32,256]{2,1,0:T(8,128)S(1)}, u32[]{:S(2)}, u32[]{:S(2)}) %collective-permute-start.3) | collective-permute-done | bytes 65568 | tf_op jit(solution)/shard_map/ppermute | solution.py:386
  25.5 0.0 collective-permute-done.refs_0_.refs_2_
  25.5 0.0 collective-permute-done.1.refs_1_.refs_3_
  25.5 9.2 %curl.2 = (f32[12,32,256]{2,1,0:T(8,128)S(1)}, f32[12,32,256]{2,1,0:T(8,128)S(1)}, f32[12,32,256]{2,1,0:T(8,128)S(1)}, f32[12,32,256]{2,1,0:T(8,128)S(1)}, f32[1...) custom-call(s32[3]{0:T(128)S(1)} %pad_add_fusion.pos, f32[3,32,96,256]{3,2,1,0:T(8,128)} %refs_1_.1, ...), custom_call_target="tpu_custom_call" | custom-call | flops 15728640 | bytes 15728640 | tf_op jit(solution)/shard_map/curl/pallas_call | solution.py:262
  34.7 0.7 collective-permute-start.14
  35.4 5.6 %collective-permute-start.16 = (f32[16,48,128]{2,1,0:T(8,128)S(1)}, f32[16,48,128]{2,1,0:T(8,128)S(1)}, u32[]{:S(2)}, u32[]{:S(2)}) collective-permute-start(f32[16,48,128]{2,1,0:T(8,128)S(1)} %get-tuple-element.40.refs_0_), channel_id=1, source_target_pairs={{0,4},{1,5},{6,2},{7,3},{8,12},{9,13},{14,10},{15,11},{16,20},{17,... | collective-permute-start | bytes 1179656 | tf_op jit(solution)/shard_map/ppermute | solution.py:371
  41.0 0.1 collective-permute-start.6
  41.1 2.4 %collective-permute-start.7 = (f32[12,32,256]{2,1,0:T(8,128)S(1)}, f32[12,32,256]{2,1,0:T(8,128)S(1)}, u32[]{:S(2)}, u32[]{:S(2)}) collective-permute-start(f32[12,32,256]{2,1,0:T(8,128)S(1)} %get-tuple-element.33), channel_id=1, source_target_pairs={{0,6},{1,7},{2,4},{3,5},{4,2},{5,3},{6,0},{7,1},{8,14},{9,15},{10,... | collective-permute-start | bytes 1179656 | tf_op jit(solution)/shard_map/ppermute | solution.py:371
  43.6 0.0 collective-permute-done.14
  43.6 1.3 collective-permute-start.15
  44.9 4.1 %collective-permute-done.16 = f32[16,48,128]{2,1,0:T(8,128)S(1)} collective-permute-done((f32[16,48,128]{2,1,0:T(8,128)S(1)}, f32[16,48,128]{2,1,0:T(8,128)S(1)}, u32[]{:S(2)}, u32[]{:S(2)}) %collective-permute-start.16) | collective-permute-done | bytes 393248 | tf_op jit(solution)/shard_map/ppermute | solution.py:371
  49.0 1.3 collective-permute-start.17
  50.3 2.4 %collective-permute-start.9 = (f32[12,32,256]{2,1,0:T(8,128)S(1)}, f32[12,32,256]{2,1,0:T(8,128)S(1)}, u32[]{:S(2)}, u32[]{:S(2)}) collective-permute-start(f32[12,32,256]{2,1,0:T(8,128)S(1)} %get-tuple-element.36), channel_id=1, source_target_pairs={{0,1},{1,0},{2,3},{3,2},{4,5},{5,4},{6,7},{7,6},{8,9},{9,8},{10,11... | collective-permute-start | bytes 1179656 | tf_op jit(solution)/shard_map/ppermute | solution.py:371
  52.7 4.6 %curl.3 = (f32[12,32,256]{2,1,0:T(8,128)S(1)}, f32[12,32,256]{2,1,0:T(8,128)S(1)}) custom-call(s32[3]{0:T(128)S(1)} %pad_add_fusion.pos, f32[3,32,96,256]{3,2,1,0:T(8,128)} %refs_1_.1, f32[3,32,96,256]{3,2,1,0:T(8,128)} %refs_1_.1, f32[3,32,96,256]{3,2,1,0:T(8,128)} %refs_1_.1, f32[3,32,96,256]{3,2,1,0:T(8,128)} %refs_1_.1, f32[3,32,96,256]{3,2,1,0:T(8,128)} %refs_1_.1, ...), custom_call_target="tpu_custom_call" | custom-call | flops 3932160 | bytes 3932160 | tf_op jit(solution)/shard_map/curl/pallas_call | solution.py:262
  57.3 0.1 collective-permute-done.6.refs_0_
  57.4 8.5 %collective-permute-start.10 = (f32[12,32,256]{2,1,0:T(8,128)S(1)}, f32[12,32,256]{2,1,0:T(8,128)S(1)}, u32[]{:S(2)}, u32[]{:S(2)}) collective-permute-start(f32[12,32,256]{2,1,0:T(8,128)S(1)} %get-tuple-element.37), channel_id=1, source_target_pairs={{0,3},{1,2},{2,1},{3,0},{4,7},{5,6},{6,5},{7,4},{8,11},{9,10},{10,... | collective-permute-start | bytes 1179656 | tf_op jit(solution)/shard_map/ppermute | solution.py:371
  65.9 2.8 %collective-permute-done.7.refs_1_ = f32[12,32,256]{2,1,0:T(8,128)S(1)} collective-permute-done((f32[12,32,256]{2,1,0:T(8,128)S(1)}, f32[12,32,256]{2,1,0:T(8,128)S(1)}, u32[]{:S(2)}, u32[]{:S(2)}) %collective-permute-start.7) | collective-permute-done | bytes 393248 | tf_op jit(solution)/shard_map/ppermute | solution.py:371
  68.7 4.9 %collective-permute-start.13 = (f32[16,48,128]{2,1,0:T(8,128)S(1)}, f32[16,48,128]{2,1,0:T(8,128)S(1)}, u32[]{:S(2)}, u32[]{:S(2)}) collective-permute-start(f32[16,48,128]{2,1,0:T(8,128)S(1)} %get-tuple-element.40.refs_0_), channel_id=1, source_target_pairs={{0,2},{1,3},{2,0},{3,1},{4,6},{5,7},{6,4},{7,5},{8,10},{9,11},{10,... | collective-permute-start | bytes 1179656 | tf_op jit(solution)/shard_map/ppermute | solution.py:371
  73.6 1.0 collective-permute-done.15
  74.6 0.5 collective-permute-start.11
  75.1 16.4 %collective-permute-done.17 = f32[16,48,128]{2,1,0:T(8,128)S(1)} collective-permute-done((f32[16,48,128]{2,1,0:T(8,128)S(1)}, f32[16,48,128]{2,1,0:T(8,128)S(1)}, u32[]{:S(2)}, u32[]{:S(2)}) %collective-permute-start.17) | collective-permute-done | bytes 393248 | tf_op jit(solution)/shard_map/ppermute | solution.py:371
  91.5 1.8 %collective-permute-start.12 = (f32[12,32,256]{2,1,0:T(8,128)S(1)}, f32[12,32,256]{2,1,0:T(8,128)S(1)}, u32[]{:S(2)}, u32[]{:S(2)}) collective-permute-start(f32[12,32,256]{2,1,0:T(8,128)S(1)} %get-tuple-element.39), channel_id=1, source_target_pairs={{0,5},{1,4},{2,7},{3,6},{4,1},{5,0},{6,3},{7,2},{8,13},{9,12},{10,... | collective-permute-start | bytes 1179656 | tf_op jit(solution)/shard_map/ppermute | solution.py:371
  93.4 0.0 collective-permute-done.9.refs_1_
  93.4 1.7 %collective-permute-start.18 = (f32[16,48,128]{2,1,0:T(8,128)S(1)}, f32[16,48,128]{2,1,0:T(8,128)S(1)}, u32[]{:S(2)}, u32[]{:S(2)}) collective-permute-start(f32[16,48,128]{2,1,0:T(8,128)S(1)} %get-tuple-element.40.refs_0_), channel_id=1, source_target_pairs={{0,1},{1,0},{2,3},{3,2},{4,5},{5,4},{6,7},{7,6},{8,9},{9,8},{10,11... | collective-permute-start | bytes 1179656 | tf_op jit(solution)/shard_map/ppermute | solution.py:371
  95.1 8.7 %collective-permute-done.10.refs_2_ = f32[12,32,256]{2,1,0:T(8,128)S(1)} collective-permute-done((f32[12,32,256]{2,1,0:T(8,128)S(1)}, f32[12,32,256]{2,1,0:T(8,128)S(1)}, u32[]{:S(2)}, u32[]{:S(2)}) %collective-permute-start.10) | collective-permute-done | bytes 393248 | tf_op jit(solution)/shard_map/ppermute | solution.py:371
  103.8 0.0 collective-permute-start.8
  103.8 21.4 %collective-permute-done.13.refs_1_ = f32[16,48,128]{2,1,0:T(8,128)S(1)} collective-permute-done((f32[16,48,128]{2,1,0:T(8,128)S(1)}, f32[16,48,128]{2,1,0:T(8,128)S(1)}, u32[]{:S(2)}, u32[]{:S(2)}) %collective-permute-start.13) | collective-permute-done | bytes 393248 | tf_op jit(solution)/shard_map/ppermute | solution.py:371
  125.2 1.9 %collective-permute-start.19 = (f32[16,48,128]{2,1,0:T(8,128)S(1)}, f32[16,48,128]{2,1,0:T(8,128)S(1)}, u32[]{:S(2)}, u32[]{:S(2)}) collective-permute-start(f32[16,48,128]{2,1,0:T(8,128)S(1)} %collective-permute-done.13.refs_1_), channel_id=1, source_target_pairs={{0,1},{1,0},{2,3},{3,2},{4,5},{5,4},{6,7},{7,6},{8,9},{9,8},{10,11... | collective-permute-start | bytes 1179656 | tf_op jit(solution)/shard_map/ppermute | solution.py:371
  127.1 0.0 collective-permute-done.11.refs_3_
  127.1 0.0 collective-permute-start.20
  127.1 0.0 collective-permute-done.12.refs_4_
  127.1 0.5 collective-permute-start.21
  127.6 1.8 %lay.2.refs_3_ = f32[12,32,2048]{2,1,0:T(8,128)} custom-call(s32[3]{0:T(128)S(1)} %pad_add_fusion.pos, f32[12,32,256]{2,1,0:T(8,128)S(1)} %get-tuple-element.35.refs_0_, f32[12,32,256]{2,1,0:T(8,128)S(1)} %collective-permute-done.9.refs_1_, f32[12,32,256]{2,1,0:T(8,128)S(1)} %collective-permute-done.10.refs_2_, ...), custom_call_target="tpu_custom_call" | custom-call | flops 491520 | bytes 3932160 | tf_op jit(solution)/shard_map/lay/pallas_call | solution.py:305
  129.4 0.0 collective-permute-done.8.refs_2_
  129.5 1.6 %lay.3 = f32[12,32,2048]{2,1,0:T(8,128)} custom-call(s32[3]{0:T(128)S(1)} %pad_add_fusion.pos, f32[12,32,256]{2,1,0:T(8,128)S(1)} %collective-permute-done.6.refs_0_, f32[12,32,256]{2,1,0:T(8,128)S(1)} %collective-permute-done.7.refs_1_, f32[12,32,256]{2,1,0:T(8,128)S(1)} %collective-permute-done.8.refs_2_, ...), custom_call_target="tpu_custom_call", output_to_operand_aliasing={{}: (4, {})} | custom-call | flops 294912 | bytes 2359296 | tf_op jit(solution)/shard_map/lay/pallas_call | solution.py:305
  131.0 0.0 collective-permute-done.18.refs_4_
  131.1 0.0 collective-permute-done.19.refs_5_
  131.1 0.0 collective-permute-done.20.refs_6_
  131.1 0.0 collective-permute-done.21.refs_7_
  131.1 3.0 %levels.1 = (f32[16,48,1024]{2,1,0:T(8,128)}, f32[8,24,512]{2,1,0:T(8,128)}, f32[12,4,256]{2,1,0:T(4,128)}, f32[6,2,128]{2,1,0:T(2,128)}, f32[3,1,64]{2,1,0:T(1,128)}) custom-call(s32[3]{0:T(128)S(1)} %pad_add_fusion.pos, f32[16,48,128]{2,1,0:T(8,128)S(1)} %get-tuple-element.40.refs_0_, f32[16,48,128]{2,1,0:T(8,128)S(1)} %collective-permute-done.13.refs_1_, ...), custom_call_target="tpu_custom_call" | custom-call | flops 3145728 | bytes 7864320 | tf_op jit(solution)/shard_map/levels/pallas_call | solution.py:356
  (2 shorter events, 0.1 us)
Async XLA Ops:
  4.1 21.3 %collective-permute-start = (f32[2,96,256]{2,1,0:T(8,128)S(1)}, f32[2,96,256]{2,1,0:T(8,128)S(1)}, u32[]{:S(2)}, u32[]{:S(2)}) collective-permute-start(f32[2,96,256]{2,1,0:T(8,128)S(1)} %get-tuple-element.26), channel_id=1, source_target_pairs={{0,64},{64,128},{128,192},{192,0},{1,65},{65,129},{129,193},{193,1... | collective-permute-start | bytes 589832 | tf_op jit(solution)/shard_map/ppermute | solution.py:386
  5.4 20.0 %collective-permute-start.1 = (f32[2,96,256]{2,1,0:T(8,128)S(1)}, f32[2,96,256]{2,1,0:T(8,128)S(1)}, u32[]{:S(2)}, u32[]{:S(2)}) collective-permute-start(f32[2,96,256]{2,1,0:T(8,128)S(1)} %get-tuple-element.27), channel_id=1, source_target_pairs={{64,0},{128,64},{192,128},{0,192},{65,1},{129,65},{193,129},{1,193... | collective-permute-start | bytes 589832 | tf_op jit(solution)/shard_map/ppermute | solution.py:386
  6.9 8.4 %collective-permute-start.4 = (f32[96,128]{1,0:T(8,128)S(1)}, f32[96,128]{1,0:T(8,128)S(1)}, u32[]{:S(2)}, u32[]{:S(2)}) collective-permute-start(f32[96,128]{1,0:T(8,128)S(1)} %get-tuple-element.30), channel_id=1, source_target_pairs={{0,1},{1,2},{2,3},{3,4},{4,5},{5,6},{6,7},{7,0},{8,9},{9,10},{10,1... | collective-permute-start | bytes 147464 | tf_op jit(solution)/shard_map/ppermute | solution.py:386
  9.7 10.5 %collective-permute-start.2 = (f32[2,32,256]{2,1,0:T(8,128)S(1)}, f32[2,32,256]{2,1,0:T(8,128)S(1)}, u32[]{:S(2)}, u32[]{:S(2)}) collective-permute-start(f32[2,32,256]{2,1,0:T(8,128)S(1)} %get-tuple-element.28), channel_id=1, source_target_pairs={{0,8},{8,16},{16,24},{24,32},{32,40},{40,48},{48,56},{56,0},{1,9},... | collective-permute-start | bytes 196616 | tf_op jit(solution)/shard_map/ppermute | solution.py:386
  15.3 10.1 %collective-permute-start.3 = (f32[2,32,256]{2,1,0:T(8,128)S(1)}, f32[2,32,256]{2,1,0:T(8,128)S(1)}, u32[]{:S(2)}, u32[]{:S(2)}) collective-permute-start(f32[2,32,256]{2,1,0:T(8,128)S(1)} %get-tuple-element.29), channel_id=1, source_target_pairs={{8,0},{16,8},{24,16},{32,24},{40,32},{48,40},{56,48},{0,56},{9,1},... | collective-permute-start | bytes 196616 | tf_op jit(solution)/shard_map/ppermute | solution.py:386
  15.3 4.9 %collective-permute-start.5 = (f32[96,128]{1,0:T(8,128)S(1)}, f32[96,128]{1,0:T(8,128)S(1)}, u32[]{:S(2)}, u32[]{:S(2)}) collective-permute-start(f32[96,128]{1,0:T(8,128)S(1)} %get-tuple-element.31), channel_id=1, source_target_pairs={{1,0},{2,1},{3,2},{4,3},{5,4},{6,5},{7,6},{0,7},{9,8},{10,9},{11,1... | collective-permute-start | bytes 147464 | tf_op jit(solution)/shard_map/ppermute | solution.py:386
  34.7 8.9 %collective-permute-start.14 = (f32[16,48,128]{2,1,0:T(8,128)S(1)}, f32[16,48,128]{2,1,0:T(8,128)S(1)}, u32[]{:S(2)}, u32[]{:S(2)}) collective-permute-start(f32[16,48,128]{2,1,0:T(8,128)S(1)} %get-tuple-element.40.refs_0_), channel_id=1, source_target_pairs={{2,4},{3,5},{4,2},{5,3},{10,12},{11,13},{12,10},{13,11},{18,20},{1... | collective-permute-start | bytes 1179656 | tf_op jit(solution)/shard_map/ppermute | solution.py:371
  35.4 13.6 %collective-permute-start.16 = (f32[16,48,128]{2,1,0:T(8,128)S(1)}, f32[16,48,128]{2,1,0:T(8,128)S(1)}, u32[]{:S(2)}, u32[]{:S(2)}) collective-permute-start(f32[16,48,128]{2,1,0:T(8,128)S(1)} %get-tuple-element.40.refs_0_), channel_id=1, source_target_pairs={{0,4},{1,5},{6,2},{7,3},{8,12},{9,13},{14,10},{15,11},{16,20},{17,... | collective-permute-start | bytes 1179656 | tf_op jit(solution)/shard_map/ppermute | solution.py:371
  41.0 16.4 %collective-permute-start.6 = (f32[12,32,256]{2,1,0:T(8,128)S(1)}, f32[12,32,256]{2,1,0:T(8,128)S(1)}, u32[]{:S(2)}, u32[]{:S(2)}) collective-permute-start(f32[12,32,256]{2,1,0:T(8,128)S(1)} %get-tuple-element.32), channel_id=1, source_target_pairs={{0,2},{1,3},{2,0},{3,1},{4,6},{5,7},{6,4},{7,5},{8,10},{9,11},{10,... | collective-permute-start | bytes 1179656 | tf_op jit(solution)/shard_map/ppermute | solution.py:371
  41.1 27.6 %collective-permute-start.7 = (f32[12,32,256]{2,1,0:T(8,128)S(1)}, f32[12,32,256]{2,1,0:T(8,128)S(1)}, u32[]{:S(2)}, u32[]{:S(2)}) collective-permute-start(f32[12,32,256]{2,1,0:T(8,128)S(1)} %get-tuple-element.33), channel_id=1, source_target_pairs={{0,6},{1,7},{2,4},{3,5},{4,2},{5,3},{6,0},{7,1},{8,14},{9,15},{10,... | collective-permute-start | bytes 1179656 | tf_op jit(solution)/shard_map/ppermute | solution.py:371
  43.6 31.0 %collective-permute-start.15 = (f32[16,48,128]{2,1,0:T(8,128)S(1)}, f32[16,48,128]{2,1,0:T(8,128)S(1)}, u32[]{:S(2)}, u32[]{:S(2)}) collective-permute-start(f32[16,48,128]{2,1,0:T(8,128)S(1)} %collective-permute-done.14), channel_id=1, source_target_pairs={{2,0},{3,1},{4,6},{5,7},{10,8},{11,9},{12,14},{13,15},{18,16},{19,... | collective-permute-start | bytes 1179656 | tf_op jit(solution)/shard_map/ppermute | solution.py:371
  49.0 42.5 %collective-permute-start.17 = (f32[16,48,128]{2,1,0:T(8,128)S(1)}, f32[16,48,128]{2,1,0:T(8,128)S(1)}, u32[]{:S(2)}, u32[]{:S(2)}) collective-permute-start(f32[16,48,128]{2,1,0:T(8,128)S(1)} %collective-permute-done.16), channel_id=1, source_target_pairs={{2,0},{3,1},{4,6},{5,7},{10,8},{11,9},{12,14},{13,15},{18,16},{19,... | collective-permute-start | bytes 1179656 | tf_op jit(solution)/shard_map/ppermute | solution.py:371
  50.3 43.1 %collective-permute-start.9 = (f32[12,32,256]{2,1,0:T(8,128)S(1)}, f32[12,32,256]{2,1,0:T(8,128)S(1)}, u32[]{:S(2)}, u32[]{:S(2)}) collective-permute-start(f32[12,32,256]{2,1,0:T(8,128)S(1)} %get-tuple-element.36), channel_id=1, source_target_pairs={{0,1},{1,0},{2,3},{3,2},{4,5},{5,4},{6,7},{7,6},{8,9},{9,8},{10,11... | collective-permute-start | bytes 1179656 | tf_op jit(solution)/shard_map/ppermute | solution.py:371
  57.4 46.3 %collective-permute-start.10 = (f32[12,32,256]{2,1,0:T(8,128)S(1)}, f32[12,32,256]{2,1,0:T(8,128)S(1)}, u32[]{:S(2)}, u32[]{:S(2)}) collective-permute-start(f32[12,32,256]{2,1,0:T(8,128)S(1)} %get-tuple-element.37), channel_id=1, source_target_pairs={{0,3},{1,2},{2,1},{3,0},{4,7},{5,6},{6,5},{7,4},{8,11},{9,10},{10,... | collective-permute-start | bytes 1179656 | tf_op jit(solution)/shard_map/ppermute | solution.py:371
  68.7 56.4 %collective-permute-start.13 = (f32[16,48,128]{2,1,0:T(8,128)S(1)}, f32[16,48,128]{2,1,0:T(8,128)S(1)}, u32[]{:S(2)}, u32[]{:S(2)}) collective-permute-start(f32[16,48,128]{2,1,0:T(8,128)S(1)} %get-tuple-element.40.refs_0_), channel_id=1, source_target_pairs={{0,2},{1,3},{2,0},{3,1},{4,6},{5,7},{6,4},{7,5},{8,10},{9,11},{10,... | collective-permute-start | bytes 1179656 | tf_op jit(solution)/shard_map/ppermute | solution.py:371
  74.6 52.5 %collective-permute-start.11 = (f32[12,32,256]{2,1,0:T(8,128)S(1)}, f32[12,32,256]{2,1,0:T(8,128)S(1)}, u32[]{:S(2)}, u32[]{:S(2)}) collective-permute-start(f32[12,32,256]{2,1,0:T(8,128)S(1)} %get-tuple-element.38), channel_id=1, source_target_pairs={{0,4},{1,5},{2,6},{3,7},{4,0},{5,1},{6,2},{7,3},{8,12},{9,13},{10,... | collective-permute-start | bytes 1179656 | tf_op jit(solution)/shard_map/ppermute | solution.py:371
  91.5 35.6 %collective-permute-start.12 = (f32[12,32,256]{2,1,0:T(8,128)S(1)}, f32[12,32,256]{2,1,0:T(8,128)S(1)}, u32[]{:S(2)}, u32[]{:S(2)}) collective-permute-start(f32[12,32,256]{2,1,0:T(8,128)S(1)} %get-tuple-element.39), channel_id=1, source_target_pairs={{0,5},{1,4},{2,7},{3,6},{4,1},{5,0},{6,3},{7,2},{8,13},{9,12},{10,... | collective-permute-start | bytes 1179656 | tf_op jit(solution)/shard_map/ppermute | solution.py:371
  93.4 37.6 %collective-permute-start.18 = (f32[16,48,128]{2,1,0:T(8,128)S(1)}, f32[16,48,128]{2,1,0:T(8,128)S(1)}, u32[]{:S(2)}, u32[]{:S(2)}) collective-permute-start(f32[16,48,128]{2,1,0:T(8,128)S(1)} %get-tuple-element.40.refs_0_), channel_id=1, source_target_pairs={{0,1},{1,0},{2,3},{3,2},{4,5},{5,4},{6,7},{7,6},{8,9},{9,8},{10,11... | collective-permute-start | bytes 1179656 | tf_op jit(solution)/shard_map/ppermute | solution.py:371
  103.8 25.7 %collective-permute-start.8 = (f32[12,32,256]{2,1,0:T(8,128)S(1)}, f32[12,32,256]{2,1,0:T(8,128)S(1)}, u32[]{:S(2)}, u32[]{:S(2)}) collective-permute-start(f32[12,32,256]{2,1,0:T(8,128)S(1)} %get-tuple-element.34), channel_id=1, source_target_pairs={{0,7},{1,6},{2,5},{3,4},{4,3},{5,2},{6,1},{7,0},{8,15},{9,14},{10,... | collective-permute-start | bytes 1179656 | tf_op jit(solution)/shard_map/ppermute | solution.py:371
  125.2 5.9 %collective-permute-start.19 = (f32[16,48,128]{2,1,0:T(8,128)S(1)}, f32[16,48,128]{2,1,0:T(8,128)S(1)}, u32[]{:S(2)}, u32[]{:S(2)}) collective-permute-start(f32[16,48,128]{2,1,0:T(8,128)S(1)} %collective-permute-done.13.refs_1_), channel_id=1, source_target_pairs={{0,1},{1,0},{2,3},{3,2},{4,5},{5,4},{6,7},{7,6},{8,9},{9,8},{10,11... | collective-permute-start | bytes 1179656 | tf_op jit(solution)/shard_map/ppermute | solution.py:371
  127.1 4.0 %collective-permute-start.20 = (f32[16,48,128]{2,1,0:T(8,128)S(1)}, f32[16,48,128]{2,1,0:T(8,128)S(1)}, u32[]{:S(2)}, u32[]{:S(2)}) collective-permute-start(f32[16,48,128]{2,1,0:T(8,128)S(1)} %add.6.refs_2_), channel_id=1, source_target_pairs={{0,1},{1,0},{2,3},{3,2},{4,5},{5,4},{6,7},{7,6},{8,9},{9,8},{10,11... | collective-permute-start | bytes 1179656 | tf_op jit(solution)/shard_map/ppermute | solution.py:371
  127.1 4.0 %collective-permute-start.21 = (f32[16,48,128]{2,1,0:T(8,128)S(1)}, f32[16,48,128]{2,1,0:T(8,128)S(1)}, u32[]{:S(2)}, u32[]{:S(2)}) collective-permute-start(f32[16,48,128]{2,1,0:T(8,128)S(1)} %add.7.refs_3_), channel_id=1, source_target_pairs={{0,1},{1,0},{2,3},{3,2},{4,5},{5,4},{6,7},{7,6},{8,9},{9,8},{10,11... | collective-permute-start | bytes 1179656 | tf_op jit(solution)/shard_map/ppermute | solution.py:371
where the time goes:
time: 134 us
  waiting for transfers between devices  64.6 us (48%)
  starting transfers between devices  44.7 us (33%)
  Pallas kernels  23.8 us (18%)
    ppermute x16, waiting for transfers between devices, send(): return lax.ppermute(value, 'gz', pairs)  54.6 us
    ppermute x16, starting transfers between devices, send(): return lax.ppermute(value, 'gz', pairs)  33.5 us
    pallas_call x2, Pallas kernels, curl(): pl.pallas_call(functools.partial(curl_kernel, shifts, each, with_level, w...  13.8 us
    ppermute x6, starting transfers between devices, exchange(): return (lax.ppermute(last, axis, up), lax.ppermute(first, axis, down))  11.2 us
    ppermute x6, waiting for transfers between devices, exchange(): return (lax.ppermute(last, axis, up), lax.ppermute(first, axis, down))  10.1 us
    pallas_call x1, Pallas kernels, ends(): pl.pallas_call(ends_kernel, in_specs=[pl.BlockSpec(memory_space=pl.ANY)],...  3.5 us
    pallas_call x2, Pallas kernels, lay(): pl.pallas_call(functools.partial(lay_kernel, shifts), in_specs=in_specs,...  3.43 us
    pallas_call x1, Pallas kernels, levels(): pl.pallas_call(levels_kernel, in_specs=[pl.BlockSpec(memory_space=pltpu.S...  3.02 us
  transfers between devices with their start and end apart: 22, of which 9 were waited for; matrix products, arithmetic and copies ran while one was open for 0% of the time, Pallas kernels for 6%

commit v1 on v0

--- a/solution.py
+++ b/solution.py
@@ -116,18 +116,19 @@
     )(velocity)
 
 
-def curl_kernel(shifts, each, with_level, which, bands, pos, vel, v_before, v_after, w_before, w_after, *refs):
-    if bands > 1:
+def curl_kernel(
+    shifts, patched, each, which, pos, vel, v_before, v_after, w_before, w_after, *refs
+):
+    count = len(shifts)
+    if patched:
+        x_before, x_after, y_before, y_after, z_before, z_after = refs[:6]
+        level_out, turned, summed = refs[-3:]
+        outs = refs[6:-3]
+        mags, strips = outs[:count], outs[count:]
+    else:
         above, below = refs[:2]
-        refs = refs[2:]
-    x_before, x_after, y_before, y_after, z_before, z_after = refs[:6]
-    count = len(shifts)
-    if with_level:
-        level_out, turned, summed = refs[-3:]
-        mags = refs[-3 - count : -3]
-    else:
         turned = refs[-1]
-        mags = refs[-1 - count : -1]
+        mags = refs[2:-1]
     band_at, me = pos[which], pos[0]
     step = pl.program_id(0)
     _, planes, rows, depth = vel.shape
@@ -135,7 +136,6 @@
     tiles = depth // 128
     lane = lax.broadcasted_iota(jnp.int32, (tall, 128), 1)
     at_first, at_last, even_lane = lane == 0, lane == 127, lane % 2 == 0
-    at_top, at_bottom = band_at == 0, band_at == bands - 1
     at_start = step == 0
     row0 = pl.multiple_of(band_at * rows, 8)
     at_end = step == pl.num_programs(0) - 1
@@ -146,7 +146,8 @@
             band = slice(lo, hi)
             both = []
             here = pl.ds(row0 + lo, tall)
-            fills = jnp.where(even_lane, z_before[here, :], z_after[here, :])
+            if patched:
+                fills = jnp.where(even_lane, z_before[here, :], z_after[here, :])
             for p in (2 * pair, 2 * pair + 1):
 
                 def first_diff(k):
@@ -154,35 +155,43 @@
                         ahead = vel[k, p + 1, band, :]
                     else:
                         near = (v_after, w_after)[k - 1][0, 0, band, :]
-                        ahead = jnp.where(at_end, x_after[k - 1, here, :], near)
+                        ahead = near
+                        if patched:
+                            ahead = jnp.where(at_end, x_after[k - 1, here, :], near)
                     if p > 0:
                         behind = vel[k, p - 1, band, :]
                     else:
                         near = (v_before, w_before)[k - 1][0, 0, band, :]
-                        behind = jnp.where(at_start, x_before[k - 1, here, :], near)
+                        behind = near
+                        if patched:
+                            behind = jnp.where(at_start, x_before[k - 1, here, :], near)
                     return ahead - behind
 
                 def second_diff(k):
                     slot = 0 if k == 0 else 1
                     if lo == 0:
-                        edge = y_before[slot, pl.ds(step * planes + p, 1), :]
-                        if bands > 1:
-                            edge = jnp.where(at_top, edge, above[k, p, 7:8, :])
+                        if patched:
+                            edge = y_before[slot, pl.ds(step * planes + p, 1), :]
+                        else:
+                            edge = above[k, p, 7:8, :]
                         behind = jnp.concatenate([edge, vel[k, p, 0 : hi - 1, :]], axis=0)
                     else:
                         behind = vel[k, p, lo - 1 : hi - 1, :]
                     if hi == rows:
-                        edge = y_after[slot, pl.ds(step * planes + p, 1), :]
-                        if bands > 1:
-                            edge = jnp.where(at_bottom, edge, below[k, p, 0:1, :])
+                        if patched:
+                            edge = y_after[slot, pl.ds(step * planes + p, 1), :]
+                        else:
+                            edge = below[k, p, 0:1, :]
                         ahead = jnp.concatenate([vel[k, p, lo + 1 : hi, :], edge], axis=0)
                     else:
                         ahead = vel[k, p, lo + 1 : hi + 1, :]
                     return ahead - behind
 
                 def third_diff(k):
-                    last, _ = lanes_at(k, step * planes + p)
-                    fill = pltpu.roll(fills, lax.rem(128 - last, 128), 1)
+                    fill = jnp.zeros((tall, 128), F32)
+                    if patched:
+                        last, _ = lanes_at(k, step * planes + p)
+                        fill = pltpu.roll(fills, lax.rem(128 - last, 128), 1)
                     parts = [vel[k, p, band, t * 128 : (t + 1) * 128] for t in range(tiles)]
                     on = [pltpu.roll(part, 127, 1) for part in parts] + [fill]
                     back = [fill] + [pltpu.roll(part, 1, 1) for part in parts]
@@ -205,9 +214,9 @@
                     turned[t, pl.ds(lo * planes + p, tall, stride=planes), :] = mag[
                         :, t * 128 : (t + 1) * 128
                     ]
-            if with_level:
+            if patched:
                 keep_rows(summed, pair * rows + lo, both[0] + both[1])
-    if with_level:
+    if patched:
         level = pair_lanes(pair_rows(summed, planes // 2 * rows // 2)) * 0.125
         level_out[...] = level.reshape(planes // 2, rows // 2, depth // 2)
     size = each * planes
@@ -217,15 +226,47 @@
         for t in range(tiles):
             for y in range(each):
                 out[y, :, t * 128 : (t + 1) * 128] = turned[t, pl.ds(at + y * planes, planes), :]
-
-
-def curl(velocity, shifts, pos, which, bands, halos, with_level=True, n=8):
+    tile_lane = lax.broadcasted_iota(jnp.int32, (planes, 128), 1)
+    for i, m in enumerate(patched):
+        ends_out, row_out = strips[2 * i : 2 * i + 2]
+        to = jnp.bitwise_xor(me, m)
+        at = pl.multiple_of(size * jnp.bitwise_and(to, mask), size)
+        edge_row = jnp.where(to == 0, 0, each - 1)
+        lanes = jnp.zeros((planes, 128), F32)
+        for y in range(each):
+            here = pl.ds(at + y * planes, planes)
+            for t, lane_to in ((0, 2 * y), (1, (2 * y + 127) % 128)):
+                moved = pltpu.roll(turned[t, here, :], 2 * y, 1) if y else turned[t, here, :]
+                lanes = jnp.where(tile_lane == lane_to, moved, lanes)
+        for k in range(4):
+
+            @pl.when(step == k)
+            def _():
+                row, col = 24 + k // 2 * 8, k % 2 * 128
+                ends_out[row : row + 8, col : col + 128] = lanes
+
+        for t in range(tiles):
+            cols = slice(t * 128, (t + 1) * 128)
+            row_out[:, cols] = turned[t, pl.ds(at + edge_row * planes, planes), :]
+            first = turned[t, pl.ds(at, each, stride=planes), :]
+            final = turned[t, pl.ds(at + planes - 1, each, stride=planes), :]
+
+            @pl.when(at_start)
+            def _():
+                ends_out[0:each, cols] = first
+
+            @pl.when(at_end)
+            def _():
+                ends_out[each : 2 * each, cols] = final
+
+
+def curl(velocity, shifts, pos, which, bands, halos=(), patched=(), n=8):
     _, X, Y, Z = velocity.shape
     H = Y // bands
     each = Y // n
     planes = PLANES
     tiles = Z // 128
-    (x_before, x_after), (y_before, y_after), (z_before, z_after) = halos
+    halos = [value for pair in halos for value in pair]
 
     def single(comp, shift):
         def index(i, pos):
@@ -247,20 +288,25 @@
         single(1, planes),
         single(2, -1),
         single(2, planes),
-        *([beside(-1), beside(H // 8)] if bands > 1 else []),
-        *[pl.BlockSpec(memory_space=pltpu.VMEM)] * 6,
+        *([] if patched else [beside(-1), beside(H // 8)]),
+        *[pl.BlockSpec(memory_space=pltpu.VMEM)] * len(halos),
     ]
-    args = [velocity] * (7 if bands > 1 else 5) + [x_before, x_after, y_before, y_after, z_before, z_after]
+    args = [velocity] * (5 if patched else 7) + halos
     out_specs = [pl.BlockSpec((each, planes, Z), lambda i, pos: (0, i, 0))] * len(shifts)
     out_shape = [jax.ShapeDtypeStruct((each, X, Z), F32)] * len(shifts)
     scratch = [pltpu.VMEM((tiles, planes * H, 128), F32)]
-    if with_level:
+    for _ in patched:
+        out_specs.append(pl.BlockSpec((40, Z), lambda i, pos: (0, 0)))
+        out_specs.append(pl.BlockSpec((planes, Z), lambda i, pos: (i, 0)))
+        out_shape.append(jax.ShapeDtypeStruct((40, Z), F32))
+        out_shape.append(jax.ShapeDtypeStruct((X, Z), F32))
+    if patched:
         out_specs.append(pl.BlockSpec((planes // 2, H // 2, Z // 2), lambda i, pos: (i, pos[which], 0)))
         out_shape.append(jax.ShapeDtypeStruct((X // 2, Y // 2, Z // 2), F32))
         scratch.append(pltpu.VMEM((tiles, planes // 2 * H, 128), F32))
     cells = X * H * Z
     return pl.pallas_call(
-        functools.partial(curl_kernel, shifts, each, with_level, which, bands),
+        functools.partial(curl_kernel, shifts, patched, each, which),
         grid_spec=pltpu.PrefetchScalarGridSpec(
             num_scalar_prefetch=1,
             grid=(X // planes,),
@@ -317,6 +363,61 @@
     )(*args)
 
 
+def patch_kernel(shifts, pos, *refs):
+    count = len(shifts)
+    blocks, strips = refs[:count], refs[count : 3 * count]
+    out, placed, away = refs[-3:]
+    each, X, depth = blocks[0].shape
+    me = pos[0]
+    lane = lax.broadcasted_iota(jnp.int32, (8, 128), 1)
+    row = lax.broadcasted_iota(jnp.int32, (8, 128), 0)
+    copies = []
+    for i, m in enumerate(shifts):
+        ends_in, row_in = strips[2 * i : 2 * i + 2]
+        for b in range(X // 8):
+            lanes = ends_in[24 + b // 2 * 8 : 32 + b // 2 * 8, b % 2 * 128 : (b % 2 + 1) * 128]
+            for y in range(each):
+                moved = pltpu.roll(lanes, 128 - 2 * y, 1) if y else lanes
+                for t in range(2):
+                    cols = slice(t * 128, (t + 1) * 128)
+                    tile = blocks[i][y, 8 * b : 8 * b + 8, cols]
+                    tile = jnp.where(lane == 127 * t, moved, tile)
+                    if b == 0:
+                        tile = jnp.where(row == 0, ends_in[y : y + 1, cols], tile)
+                    if b == X // 8 - 1:
+                        tile = jnp.where(row == 7, ends_in[each + y : each + y + 1, cols], tile)
+                    if y == 0:
+                        tile = jnp.where(me == 0, row_in[8 * b : 8 * b + 8, cols], tile)
+                    if y == each - 1:
+                        tile = jnp.where(me == 7, row_in[8 * b : 8 * b + 8, cols], tile)
+                    placed[i, y, 8 * b : 8 * b + 8, cols] = tile
+        at = pl.multiple_of(jnp.bitwise_xor(me, m) * depth, depth)
+        copy = pltpu.make_async_copy(placed.at[i], out.at[:, :, pl.ds(at, depth)], away.at[i])
+        copy.start()
+        copies.append(copy)
+    for copy in copies:
+        copy.wait()
+
+
+def patch(blocks, strips, shifts, pos, pencil, n=8):
+    each, X, Z = blocks[0].shape
+    count = len(shifts)
+    vmem, anywhere = pl.BlockSpec(memory_space=pltpu.VMEM), pl.BlockSpec(memory_space=pl.ANY)
+    return pl.pallas_call(
+        functools.partial(patch_kernel, shifts),
+        in_specs=[pl.BlockSpec(memory_space=pltpu.SMEM)] + [vmem] * (3 * count) + [anywhere],
+        out_specs=anywhere,
+        out_shape=jax.ShapeDtypeStruct((each, X, n * Z), F32),
+        scratch_shapes=[pltpu.VMEM((count, each, X, Z), F32), pltpu.SemaphoreType.DMA((count,))],
+        input_output_aliases={3 * count + 1: 0},
+        compiler_params=pltpu.CompilerParams(vmem_limit_bytes=8 << 20),
+        cost_estimate=pl.CostEstimate(
+            flops=8 * count * each * X * Z, bytes_accessed=8 * count * each * X * Z, transcendentals=0
+        ),
+        name="patch",
+    )(pos, *blocks, *strips, pencil)
+
+
 def levels_kernel(pos, *refs):
     blocks = refs[:8]
     one, two, three, four, five, s1, s2, s3, s4 = refs[8:]
@@ -389,14 +490,16 @@
 def on_device(velocity):
     at = lax.axis_index("gz").astype(jnp.int32)
     pos = jnp.stack([at, lax.shift_right_logical(at, jnp.int32(1)) ^ 2, jnp.int32(0)])
+    blocks = {}
+    blocks[4], blocks[5] = curl(velocity, (4, 5), pos, 1, 4)
     x_first, x_last, y_first, y_last, z_first, z_last = ends(velocity)
     y_halo = exchange(y_first, y_last, "gy")
     x_halo = exchange(x_first, x_last, "gx")
     z_halo = exchange(z_first, z_last, "gz")
     halos = (x_halo, y_halo, z_halo)
-    blocks = {}
-    blocks[4], blocks[5] = curl(velocity, (4, 5), pos, 1, 4, halos, with_level=False)
-    *rest, level = curl(velocity, (0, 1, 2, 3, 6, 7), pos, 2, 1, halos)
+    *rest, ends_4, row_4, ends_5, row_5, level = curl(
+        velocity, (0, 1, 2, 3, 6, 7), pos, 2, 1, halos, (4, 5)
+    )
     blocks.update(zip((0, 1, 2, 3, 6, 7), rest))
     side = swap(level, 2)
     across = [(1, 2), (2, 1)]
@@ -410,15 +513,18 @@
     got = {0: blocks[0]}
     for m in range(1, 8):
         got[m] = swap(blocks[m], m)
+    strips = [
+        swap(ends_4, 4),
+        send(row_4, [(4, 0), (3, 7)]),
+        swap(ends_5, 5),
+        send(row_5, [(5, 0), (2, 7)]),
+    ]
     upper = levels([*mine, *theirs], pos)
     upper = [*upper[:2]] + [jnp.transpose(value, (1, 0, 2)) for value in upper[2:]]
-    pencil = None
-    for which in LAYS:
-        pencil = lay([got[m] for m in which], which, pos, pencil)
+    pencil = lay([got[m] for m in (0, 1, 3)], (0, 1, 3), pos)
+    pencil = patch([got[4], got[5]], strips, (4, 5), pos, pencil)
+    pencil = lay([got[m] for m in (2, 6, 7)], (2, 6, 7), pos, pencil)
     return (jnp.transpose(pencil, (1, 0, 2)), *upper)
-
-
-LAYS = ((0, 1, 3, 4, 5), (2, 6, 7))
 
 
 def solution(mesh):

time: 134 us -> 161 us (1.20)
  starting transfers between devices: 44.7 us -> 83.2 us
  waiting for transfers between devices: 64.6 us -> 51.1 us
  Pallas kernels: 23.8 us -> 25.6 us
    ppermute x16 -> x20, starting transfers between devices: 33.5 us -> 72.1 us  [send(): return lax.ppermute(value, 'gz', pairs)]
    ppermute x16 -> x20, waiting for transfers between devices: 54.6 us -> 41 us  [send(): return lax.ppermute(value, 'gz', pairs)]
    pallas_call x2 -> x3, Pallas kernels: 13.8 us -> 15.9 us  [the longest x2 14.4 us: curl(): pl.pallas_call(functools.partial(curl_kernel, shifts, patched, each, whic...]
  transfers between devices with their start and end apart: 22 -> 26, of which waited for: 9 -> 8; matrix products, arithmetic and copies ran while one was open for 0% -> 0% of each run, Pallas kernels for 6% -> 6%
where the time goes in v1:
time: 161 us
  starting transfers between devices  83.2 us (52%)
  waiting for transfers between devices  51.1 us (32%)
  Pallas kernels  25.6 us (16%)
    ppermute x20, starting transfers between devices, send(): return lax.ppermute(value, 'gz', pairs)  72.1 us
    ppermute x20, waiting for transfers between devices, send(): return lax.ppermute(value, 'gz', pairs)  41 us
    pallas_call x2, Pallas kernels, curl(): pl.pallas_call(functools.partial(curl_kernel, shifts, patched, each, whic...  14.4 us
    ppermute x6, starting transfers between devices, exchange(): return (lax.ppermute(last, axis, up), lax.ppermute(first, axis, down))  11.2 us
    ppermute x6, waiting for transfers between devices, exchange(): return (lax.ppermute(last, axis, up), lax.ppermute(first, axis, down))  10.1 us
    pallas_call x1, Pallas kernels, ends(): pl.pallas_call(ends_kernel, in_specs=[pl.BlockSpec(memory_space=pl.ANY)],...  3.5 us
  transfers between devices with their start and end apart: 26, of which 8 were waited for; matrix products, arithmetic and copies ran while one was open for 0% of the time, Pallas kernels for 6%

profile of v1, /device:TPU:25, one launch (start us, length us, event | category | flops | bytes accessed | tf_op | source)
XLA Modules:
  0.0 160.9 jit_solution(7344658460680910147)
XLA Ops:
  0.6 3.5 %ends.1 = (f32[2,96,256]{2,1,0:T(8,128)S(1)}, f32[2,96,256]{2,1,0:T(8,128)S(1)}, f32[2,32,256]{2,1,0:T(8,128)S(1)}, f32[2,32,256]{2,1,0:T(8,128)S(1)}, f32[96,128]{1,0:T(8,128)S(1)}, /*index=5*/f32[96,128]{1,0:T(8,128)S(1)}) custom-call(f32[3,32,96,256]{3,2,1,0:T(8,128)} %refs_1_.1), custom_call_target="tpu_custom_call" | custom-call | flops 4000000 | bytes 8000000 | tf_op jit(solution)/shard_map/ends/pallas_call | solution.py:102
  4.1 1.3 collective-permute-start
  5.4 1.5 collective-permute-start.1
  6.9 2.8 %collective-permute-start.4 = (f32[96,128]{1,0:T(8,128)S(1)}, f32[96,128]{1,0:T(8,128)S(1)}, u32[]{:S(2)}, u32[]{:S(2)}) collective-permute-start(f32[96,128]{1,0:T(8,128)S(1)} %get-tuple-element.34), channel_id=1, source_target_pairs={{0,1},{1,2},{2,3},{3,4},{4,5},{5,6},{6,7},{7,0},{8,9},{9,10},{10,1... | collective-permute-start | bytes 147464 | tf_op jit(solution)/shard_map/ppermute | solution.py:487
  9.7 5.7 %collective-permute-start.2 = (f32[2,32,256]{2,1,0:T(8,128)S(1)}, f32[2,32,256]{2,1,0:T(8,128)S(1)}, u32[]{:S(2)}, u32[]{:S(2)}) collective-permute-start(f32[2,32,256]{2,1,0:T(8,128)S(1)} %get-tuple-element.32), channel_id=1, source_target_pairs={{0,8},{8,16},{16,24},{24,32},{32,40},{40,48},{48,56},{56,0},{1,9},... | collective-permute-start | bytes 196616 | tf_op jit(solution)/shard_map/ppermute | solution.py:487
  15.3 0.0 collective-permute-start.3
  15.3 0.0 collective-permute-done.4.refs_4_
  15.3 0.0 collective-permute-start.5
  15.3 0.1 pad_add_fusion.pos
  15.4 4.8 %collective-permute-done.5.refs_5_ = f32[96,128]{1,0:T(8,128)S(1)} collective-permute-done((f32[96,128]{1,0:T(8,128)S(1)}, f32[96,128]{1,0:T(8,128)S(1)}, u32[]{:S(2)}, u32[]{:S(2)}) %collective-permute-start.5) | collective-permute-done | bytes 49184 | tf_op jit(solution)/shard_map/ppermute | solution.py:487
  20.2 0.0 collective-permute-done.2.refs_2_
  20.2 5.3 %collective-permute-done.3.refs_3_ = f32[2,32,256]{2,1,0:T(8,128)S(1)} collective-permute-done((f32[2,32,256]{2,1,0:T(8,128)S(1)}, f32[2,32,256]{2,1,0:T(8,128)S(1)}, u32[]{:S(2)}, u32[]{:S(2)}) %collective-permute-start.3) | collective-permute-done | bytes 65568 | tf_op jit(solution)/shard_map/ppermute | solution.py:487
  25.5 0.0 collective-permute-done.refs_0_
  25.5 0.0 collective-permute-done.1.refs_1_
  25.5 9.9 %curl.2 = (f32[12,32,256]{2,1,0:T(8,128)S(1)}, f32[12,32,256]{2,1,0:T(8,128)S(1)}, f32[12,32,256]{2,1,0:T(8,128)S(1)}, f32[12,32,256]{2,1,0:T(8,128)S(1)}, f32[1...) custom-call(s32[3]{0:T(128)S(1)} %pad_add_fusion.pos, ...), custom_call_target="tpu_custom_call" | custom-call | flops 15728640 | bytes 15728640 | tf_op jit(solution)/shard_map/curl/pallas_call | solution.py:308
  35.4 0.7 collective-permute-start.18
  36.1 5.6 %collective-permute-start.20 = (f32[16,48,128]{2,1,0:T(8,128)S(1)}, f32[16,48,128]{2,1,0:T(8,128)S(1)}, u32[]{:S(2)}, u32[]{:S(2)}) collective-permute-start(f32[16,48,128]{2,1,0:T(8,128)S(1)} %get-tuple-element.48.refs_0_), channel_id=1, source_target_pairs={{0,4},{1,5},{6,2},{7,3},{8,12},{9,13},{14,10},{15,11},{16,20},{17,... | collective-permute-start | bytes 1179656 | tf_op jit(solution)/shard_map/ppermute | solution.py:472
  41.8 4.4 %curl.3 = (f32[12,32,256]{2,1,0:T(8,128)S(1)}, f32[12,32,256]{2,1,0:T(8,128)S(1)}) custom-call(s32[3]{0:T(128)S(1)} %pad_add_fusion.pos, f32[3,32,96,256]{3,2,1,0:T(8,128)} %refs_1_.1, f32[3,32,96,256]{3,2,1,0:T(8,128)} %refs_1_.1, f32[3,32,96,256]{3,2,1,0:T(8,128)} %refs_1_.1, f32[3,32,96,256]{3,2,1,0:T(8,128)} %refs_1_.1, f32[3,32,96,256]{3,2,1,0:T(8,128)} %refs_1_.1, ...), custom_call_target="tpu_custom_call" | custom-call | flops 3932160 | bytes 3932160 | tf_op jit(solution)/shard_map/curl/pallas_call | solution.py:308
  46.2 0.1 collective-permute-start.9
  46.3 3.3 %collective-permute-start.10 = (f32[12,32,256]{2,1,0:T(8,128)S(1)}, f32[12,32,256]{2,1,0:T(8,128)S(1)}, u32[]{:S(2)}, u32[]{:S(2)}) collective-permute-start(f32[12,32,256]{2,1,0:T(8,128)S(1)} %get-tuple-element.40), channel_id=1, source_target_pairs={{0,5},{1,4},{2,7},{3,6},{4,1},{5,0},{6,3},{7,2},{8,13},{9,12},{10,... | collective-permute-start | bytes 1179656 | tf_op jit(solution)/shard_map/ppermute | solution.py:472
  49.6 0.0 collective-permute-done.18
  49.6 1.3 collective-permute-start.19
  50.9 0.0 collective-permute-done.20
  50.9 1.3 collective-permute-start.21
  52.2 0.7 collective-permute-start.12
  52.9 0.0 collective-permute-done.12.refs_3_
  52.9 0.7 collective-permute-start.14
  53.5 0.0 collective-permute-done.14.refs_5_
  53.5 44.1 %collective-permute-start.11 = (f32[40,256]{1,0:T(8,128)S(1)}, f32[40,256]{1,0:T(8,128)S(1)}, u32[]{:S(2)}, u32[]{:S(2)}) collective-permute-start(f32[40,256]{1,0:T(8,128)S(1)} %get-tuple-element.41), channel_id=1, source_target_pairs={{0,4},{1,5},{2,6},{3,7},{4,0},{5,1},{6,2},{7,3},{8,12},{9,13},{10,... | collective-permute-start | bytes 122888 | tf_op jit(solution)/shard_map/ppermute | solution.py:472
  97.6 1.5 collective-permute-done.11.refs_2_
  99.1 4.2 %collective-permute-start.13 = (f32[40,256]{1,0:T(8,128)S(1)}, f32[40,256]{1,0:T(8,128)S(1)}, u32[]{:S(2)}, u32[]{:S(2)}) collective-permute-start(f32[40,256]{1,0:T(8,128)S(1)} %get-tuple-element.43), channel_id=1, source_target_pairs={{0,5},{1,4},{2,7},{3,6},{4,1},{5,0},{6,3},{7,2},{8,13},{9,12},{10,... | collective-permute-start | bytes 122888 | tf_op jit(solution)/shard_map/ppermute | solution.py:472
  103.3 1.8 %collective-permute-done.13.refs_4_ = f32[40,256]{1,0:T(8,128)S(1)} collective-permute-done((f32[40,256]{1,0:T(8,128)S(1)}, f32[40,256]{1,0:T(8,128)S(1)}, u32[]{:S(2)}, u32[]{:S(2)}) %collective-permute-start.13) | collective-permute-done | bytes 40992 | tf_op jit(solution)/shard_map/ppermute | solution.py:472
  105.1 0.7 collective-permute-start.6
  105.7 0.0 collective-permute-done.9.refs_0_
  105.7 3.1 %collective-permute-start.7 = (f32[12,32,256]{2,1,0:T(8,128)S(1)}, f32[12,32,256]{2,1,0:T(8,128)S(1)}, u32[]{:S(2)}, u32[]{:S(2)}) collective-permute-start(f32[12,32,256]{2,1,0:T(8,128)S(1)} %get-tuple-element.37), channel_id=1, source_target_pairs={{0,6},{1,7},{2,4},{3,5},{4,2},{5,3},{6,0},{7,1},{8,14},{9,15},{10,... | collective-permute-start | bytes 1179656 | tf_op jit(solution)/shard_map/ppermute | solution.py:472
  108.8 0.0 collective-permute-done.10.refs_1_
  108.8 0.6 collective-permute-start.17
  109.4 0.0 collective-permute-done.19
  109.4 0.8 collective-permute-start.15
  110.2 0.6 collective-permute-done.21
  110.8 0.4 collective-permute-start.16
  111.3 16.0 %collective-permute-done.6.refs_0_ = f32[12,32,256]{2,1,0:T(8,128)S(1)} collective-permute-done((f32[12,32,256]{2,1,0:T(8,128)S(1)}, f32[12,32,256]{2,1,0:T(8,128)S(1)}, u32[]{:S(2)}, u32[]{:S(2)}) %collective-permute-start.6) | collective-permute-done | bytes 393248 | tf_op jit(solution)/shard_map/ppermute | solution.py:472
  127.3 1.2 collective-permute-start.22
  128.5 0.0 collective-permute-done.7.refs_1_
  128.5 2.0 %collective-permute-start.8 = (f32[12,32,256]{2,1,0:T(8,128)S(1)}, f32[12,32,256]{2,1,0:T(8,128)S(1)}, u32[]{:S(2)}, u32[]{:S(2)}) collective-permute-start(f32[12,32,256]{2,1,0:T(8,128)S(1)} %get-tuple-element.38), channel_id=1, source_target_pairs={{0,7},{1,6},{2,5},{3,4},{4,3},{5,2},{6,1},{7,0},{8,15},{9,14},{10,... | collective-permute-start | bytes 1179656 | tf_op jit(solution)/shard_map/ppermute | solution.py:472
  130.5 5.3 %collective-permute-done.17.refs_1_ = f32[16,48,128]{2,1,0:T(8,128)S(1)} collective-permute-done((f32[16,48,128]{2,1,0:T(8,128)S(1)}, f32[16,48,128]{2,1,0:T(8,128)S(1)}, u32[]{:S(2)}, u32[]{:S(2)}) %collective-permute-start.17) | collective-permute-done | bytes 393248 | tf_op jit(solution)/shard_map/ppermute | solution.py:472
  135.8 1.1 collective-permute-start.23
  136.9 0.0 collective-permute-done.15.refs_1_
  136.9 0.0 collective-permute-start.24
  137.0 15.8 %collective-permute-done.16.refs_2_ = f32[12,32,256]{2,1,0:T(8,128)S(1)} collective-permute-done((f32[12,32,256]{2,1,0:T(8,128)S(1)}, f32[12,32,256]{2,1,0:T(8,128)S(1)}, u32[]{:S(2)}, u32[]{:S(2)}) %collective-permute-start.16) | collective-permute-done | bytes 393248 | tf_op jit(solution)/shard_map/ppermute | solution.py:472
  152.8 0.3 collective-permute-start.25
  153.1 1.6 lay.2.refs_6_
  154.7 1.6 patch.1.refs_3_
  156.2 0.0 collective-permute-done.8.refs_2_
  156.2 1.6 lay.3
  157.8 0.0 collective-permute-done.22.refs_4_
  157.8 0.0 collective-permute-done.23.refs_5_
  157.8 0.0 collective-permute-done.24.refs_6_
  157.9 0.0 collective-permute-done.25.refs_7_
  157.9 3.0 %levels.1 = (f32[16,48,1024]{2,1,0:T(8,128)}, f32[8,24,512]{2,1,0:T(8,128)}, f32[12,4,256]{2,1,0:T(4,128)}, f32[6,2,128]{2,1,0:T(2,128)}, f32[3,1,64]{2,1,0:T(1,128)}) custom-call(s32[3]{0:T(128)S(1)} %pad_add_fusion.pos, f32[16,48,128]{2,1,0:T(8,128)S(1)} %get-tuple-element.48.refs_0_, f32[16,48,128]{2,1,0:T(8,128)S(1)} %collective-permute-done.17.refs_1_, ...), custom_call_target="tpu_custom_call" | custom-call | flops 3145728 | bytes 7864320 | tf_op jit(solution)/shard_map/levels/pallas_call | solution.py:457
  (2 shorter events, 0.1 us)
Async XLA Ops:
  4.1 21.3 %collective-permute-start = (f32[2,96,256]{2,1,0:T(8,128)S(1)}, f32[2,96,256]{2,1,0:T(8,128)S(1)}, u32[]{:S(2)}, u32[]{:S(2)}) collective-permute-start(f32[2,96,256]{2,1,0:T(8,128)S(1)} %get-tuple-element.30), channel_id=1, source_target_pairs={{0,64},{64,128},{128,192},{192,0},{1,65},{65,129},{129,193},{193,1... | collective-permute-start | bytes 589832 | tf_op jit(solution)/shard_map/ppermute | solution.py:487
  5.4 20.0 %collective-permute-start.1 = (f32[2,96,256]{2,1,0:T(8,128)S(1)}, f32[2,96,256]{2,1,0:T(8,128)S(1)}, u32[]{:S(2)}, u32[]{:S(2)}) collective-permute-start(f32[2,96,256]{2,1,0:T(8,128)S(1)} %get-tuple-element.31), channel_id=1, source_target_pairs={{64,0},{128,64},{192,128},{0,192},{65,1},{129,65},{193,129},{1,193... | collective-permute-start | bytes 589832 | tf_op jit(solution)/shard_map/ppermute | solution.py:487
  6.9 8.4 %collective-permute-start.4 = (f32[96,128]{1,0:T(8,128)S(1)}, f32[96,128]{1,0:T(8,128)S(1)}, u32[]{:S(2)}, u32[]{:S(2)}) collective-permute-start(f32[96,128]{1,0:T(8,128)S(1)} %get-tuple-element.34), channel_id=1, source_target_pairs={{0,1},{1,2},{2,3},{3,4},{4,5},{5,6},{6,7},{7,0},{8,9},{9,10},{10,1... | collective-permute-start | bytes 147464 | tf_op jit(solution)/shard_map/ppermute | solution.py:487
  9.7 10.5 %collective-permute-start.2 = (f32[2,32,256]{2,1,0:T(8,128)S(1)}, f32[2,32,256]{2,1,0:T(8,128)S(1)}, u32[]{:S(2)}, u32[]{:S(2)}) collective-permute-start(f32[2,32,256]{2,1,0:T(8,128)S(1)} %get-tuple-element.32), channel_id=1, source_target_pairs={{0,8},{8,16},{16,24},{24,32},{32,40},{40,48},{48,56},{56,0},{1,9},... | collective-permute-start | bytes 196616 | tf_op jit(solution)/shard_map/ppermute | solution.py:487
  15.3 10.1 %collective-permute-start.3 = (f32[2,32,256]{2,1,0:T(8,128)S(1)}, f32[2,32,256]{2,1,0:T(8,128)S(1)}, u32[]{:S(2)}, u32[]{:S(2)}) collective-permute-start(f32[2,32,256]{2,1,0:T(8,128)S(1)} %get-tuple-element.33), channel_id=1, source_target_pairs={{8,0},{16,8},{24,16},{32,24},{40,32},{48,40},{56,48},{0,56},{9,1},... | collective-permute-start | bytes 196616 | tf_op jit(solution)/shard_map/ppermute | solution.py:487
  15.3 4.9 %collective-permute-start.5 = (f32[96,128]{1,0:T(8,128)S(1)}, f32[96,128]{1,0:T(8,128)S(1)}, u32[]{:S(2)}, u32[]{:S(2)}) collective-permute-start(f32[96,128]{1,0:T(8,128)S(1)} %get-tuple-element.35), channel_id=1, source_target_pairs={{1,0},{2,1},{3,2},{4,3},{5,4},{6,5},{7,6},{0,7},{9,8},{10,9},{11,1... | collective-permute-start | bytes 147464 | tf_op jit(solution)/shard_map/ppermute | solution.py:487
  35.4 14.2 %collective-permute-start.18 = (f32[16,48,128]{2,1,0:T(8,128)S(1)}, f32[16,48,128]{2,1,0:T(8,128)S(1)}, u32[]{:S(2)}, u32[]{:S(2)}) collective-permute-start(f32[16,48,128]{2,1,0:T(8,128)S(1)} %get-tuple-element.48.refs_0_), channel_id=1, source_target_pairs={{2,4},{3,5},{4,2},{5,3},{10,12},{11,13},{12,10},{13,11},{18,20},{1... | collective-permute-start | bytes 1179656 | tf_op jit(solution)/shard_map/ppermute | solution.py:472
  36.1 14.8 %collective-permute-start.20 = (f32[16,48,128]{2,1,0:T(8,128)S(1)}, f32[16,48,128]{2,1,0:T(8,128)S(1)}, u32[]{:S(2)}, u32[]{:S(2)}) collective-permute-start(f32[16,48,128]{2,1,0:T(8,128)S(1)} %get-tuple-element.48.refs_0_), channel_id=1, source_target_pairs={{0,4},{1,5},{6,2},{7,3},{8,12},{9,13},{14,10},{15,11},{16,20},{17,... | collective-permute-start | bytes 1179656 | tf_op jit(solution)/shard_map/ppermute | solution.py:472
  46.2 59.5 %collective-permute-start.9 = (f32[12,32,256]{2,1,0:T(8,128)S(1)}, f32[12,32,256]{2,1,0:T(8,128)S(1)}, u32[]{:S(2)}, u32[]{:S(2)}) collective-permute-start(f32[12,32,256]{2,1,0:T(8,128)S(1)} %get-tuple-element.39), channel_id=1, source_target_pairs={{0,4},{1,5},{2,6},{3,7},{4,0},{5,1},{6,2},{7,3},{8,12},{9,13},{10,... | collective-permute-start | bytes 1179656 | tf_op jit(solution)/shard_map/ppermute | solution.py:472
  46.3 62.5 %collective-permute-start.10 = (f32[12,32,256]{2,1,0:T(8,128)S(1)}, f32[12,32,256]{2,1,0:T(8,128)S(1)}, u32[]{:S(2)}, u32[]{:S(2)}) collective-permute-start(f32[12,32,256]{2,1,0:T(8,128)S(1)} %get-tuple-element.40), channel_id=1, source_target_pairs={{0,5},{1,4},{2,7},{3,6},{4,1},{5,0},{6,3},{7,2},{8,13},{9,12},{10,... | collective-permute-start | bytes 1179656 | tf_op jit(solution)/shard_map/ppermute | solution.py:472
  49.6 59.8 %collective-permute-start.19 = (f32[16,48,128]{2,1,0:T(8,128)S(1)}, f32[16,48,128]{2,1,0:T(8,128)S(1)}, u32[]{:S(2)}, u32[]{:S(2)}) collective-permute-start(f32[16,48,128]{2,1,0:T(8,128)S(1)} %collective-permute-done.18), channel_id=1, source_target_pairs={{2,0},{3,1},{4,6},{5,7},{10,8},{11,9},{12,14},{13,15},{18,16},{19,... | collective-permute-start | bytes 1179656 | tf_op jit(solution)/shard_map/ppermute | solution.py:472
  50.9 59.9 %collective-permute-start.21 = (f32[16,48,128]{2,1,0:T(8,128)S(1)}, f32[16,48,128]{2,1,0:T(8,128)S(1)}, u32[]{:S(2)}, u32[]{:S(2)}) collective-permute-start(f32[16,48,128]{2,1,0:T(8,128)S(1)} %collective-permute-done.20), channel_id=1, source_target_pairs={{2,0},{3,1},{4,6},{5,7},{10,8},{11,9},{12,14},{13,15},{18,16},{19,... | collective-permute-start | bytes 1179656 | tf_op jit(solution)/shard_map/ppermute | solution.py:472
  52.2 0.7 collective-permute-start.12
  52.9 0.7 collective-permute-start.14
  53.5 45.6 %collective-permute-start.11 = (f32[40,256]{1,0:T(8,128)S(1)}, f32[40,256]{1,0:T(8,128)S(1)}, u32[]{:S(2)}, u32[]{:S(2)}) collective-permute-start(f32[40,256]{1,0:T(8,128)S(1)} %get-tuple-element.41), channel_id=1, source_target_pairs={{0,4},{1,5},{2,6},{3,7},{4,0},{5,1},{6,2},{7,3},{8,12},{9,13},{10,... | collective-permute-start | bytes 122888 | tf_op jit(solution)/shard_map/ppermute | solution.py:472
  99.1 6.0 %collective-permute-start.13 = (f32[40,256]{1,0:T(8,128)S(1)}, f32[40,256]{1,0:T(8,128)S(1)}, u32[]{:S(2)}, u32[]{:S(2)}) collective-permute-start(f32[40,256]{1,0:T(8,128)S(1)} %get-tuple-element.43), channel_id=1, source_target_pairs={{0,5},{1,4},{2,7},{3,6},{4,1},{5,0},{6,3},{7,2},{8,13},{9,12},{10,... | collective-permute-start | bytes 122888 | tf_op jit(solution)/shard_map/ppermute | solution.py:472
  105.1 22.2 %collective-permute-start.6 = (f32[12,32,256]{2,1,0:T(8,128)S(1)}, f32[12,32,256]{2,1,0:T(8,128)S(1)}, u32[]{:S(2)}, u32[]{:S(2)}) collective-permute-start(f32[12,32,256]{2,1,0:T(8,128)S(1)} %get-tuple-element.36), channel_id=1, source_target_pairs={{0,2},{1,3},{2,0},{3,1},{4,6},{5,7},{6,4},{7,5},{8,10},{9,11},{10,... | collective-permute-start | bytes 1179656 | tf_op jit(solution)/shard_map/ppermute | solution.py:472
  105.7 22.8 %collective-permute-start.7 = (f32[12,32,256]{2,1,0:T(8,128)S(1)}, f32[12,32,256]{2,1,0:T(8,128)S(1)}, u32[]{:S(2)}, u32[]{:S(2)}) collective-permute-start(f32[12,32,256]{2,1,0:T(8,128)S(1)} %get-tuple-element.37), channel_id=1, source_target_pairs={{0,6},{1,7},{2,4},{3,5},{4,2},{5,3},{6,0},{7,1},{8,14},{9,15},{10,... | collective-permute-start | bytes 1179656 | tf_op jit(solution)/shard_map/ppermute | solution.py:472
  108.8 27.0 %collective-permute-start.17 = (f32[16,48,128]{2,1,0:T(8,128)S(1)}, f32[16,48,128]{2,1,0:T(8,128)S(1)}, u32[]{:S(2)}, u32[]{:S(2)}) collective-permute-start(f32[16,48,128]{2,1,0:T(8,128)S(1)} %get-tuple-element.48.refs_0_), channel_id=1, source_target_pairs={{0,2},{1,3},{2,0},{3,1},{4,6},{5,7},{6,4},{7,5},{8,10},{9,11},{10,... | collective-permute-start | bytes 1179656 | tf_op jit(solution)/shard_map/ppermute | solution.py:472
  109.4 27.5 %collective-permute-start.15 = (f32[12,32,256]{2,1,0:T(8,128)S(1)}, f32[12,32,256]{2,1,0:T(8,128)S(1)}, u32[]{:S(2)}, u32[]{:S(2)}) collective-permute-start(f32[12,32,256]{2,1,0:T(8,128)S(1)} %get-tuple-element.46), channel_id=1, source_target_pairs={{0,1},{1,0},{2,3},{3,2},{4,5},{5,4},{6,7},{7,6},{8,9},{9,8},{10,11... | collective-permute-start | bytes 1179656 | tf_op jit(solution)/shard_map/ppermute | solution.py:472
  110.8 41.9 %collective-permute-start.16 = (f32[12,32,256]{2,1,0:T(8,128)S(1)}, f32[12,32,256]{2,1,0:T(8,128)S(1)}, u32[]{:S(2)}, u32[]{:S(2)}) collective-permute-start(f32[12,32,256]{2,1,0:T(8,128)S(1)} %get-tuple-element.47), channel_id=1, source_target_pairs={{0,3},{1,2},{2,1},{3,0},{4,7},{5,6},{6,5},{7,4},{8,11},{9,10},{10,... | collective-permute-start | bytes 1179656 | tf_op jit(solution)/shard_map/ppermute | solution.py:472
  127.3 30.5 %collective-permute-start.22 = (f32[16,48,128]{2,1,0:T(8,128)S(1)}, f32[16,48,128]{2,1,0:T(8,128)S(1)}, u32[]{:S(2)}, u32[]{:S(2)}) collective-permute-start(f32[16,48,128]{2,1,0:T(8,128)S(1)} %get-tuple-element.48.refs_0_), channel_id=1, source_target_pairs={{0,1},{1,0},{2,3},{3,2},{4,5},{5,4},{6,7},{7,6},{8,9},{9,8},{10,11... | collective-permute-start | bytes 1179656 | tf_op jit(solution)/shard_map/ppermute | solution.py:472
  128.5 27.7 %collective-permute-start.8 = (f32[12,32,256]{2,1,0:T(8,128)S(1)}, f32[12,32,256]{2,1,0:T(8,128)S(1)}, u32[]{:S(2)}, u32[]{:S(2)}) collective-permute-start(f32[12,32,256]{2,1,0:T(8,128)S(1)} %get-tuple-element.38), channel_id=1, source_target_pairs={{0,7},{1,6},{2,5},{3,4},{4,3},{5,2},{6,1},{7,0},{8,15},{9,14},{10,... | collective-permute-start | bytes 1179656 | tf_op jit(solution)/shard_map/ppermute | solution.py:472
  135.8 22.0 %collective-permute-start.23 = (f32[16,48,128]{2,1,0:T(8,128)S(1)}, f32[16,48,128]{2,1,0:T(8,128)S(1)}, u32[]{:S(2)}, u32[]{:S(2)}) collective-permute-start(f32[16,48,128]{2,1,0:T(8,128)S(1)} %collective-permute-done.17.refs_1_), channel_id=1, source_target_pairs={{0,1},{1,0},{2,3},{3,2},{4,5},{5,4},{6,7},{7,6},{8,9},{9,8},{10,11... | collective-permute-start | bytes 1179656 | tf_op jit(solution)/shard_map/ppermute | solution.py:472
  136.9 20.9 %collective-permute-start.24 = (f32[16,48,128]{2,1,0:T(8,128)S(1)}, f32[16,48,128]{2,1,0:T(8,128)S(1)}, u32[]{:S(2)}, u32[]{:S(2)}) collective-permute-start(f32[16,48,128]{2,1,0:T(8,128)S(1)} %add.6.refs_2_), channel_id=1, source_target_pairs={{0,1},{1,0},{2,3},{3,2},{4,5},{5,4},{6,7},{7,6},{8,9},{9,8},{10,11... | collective-permute-start | bytes 1179656 | tf_op jit(solution)/shard_map/ppermute | solution.py:472
  152.8 5.1 %collective-permute-start.25 = (f32[16,48,128]{2,1,0:T(8,128)S(1)}, f32[16,48,128]{2,1,0:T(8,128)S(1)}, u32[]{:S(2)}, u32[]{:S(2)}) collective-permute-start(f32[16,48,128]{2,1,0:T(8,128)S(1)} %add.7.refs_3_), channel_id=1, source_target_pairs={{0,1},{1,0},{2,3},{3,2},{4,5},{5,4},{6,7},{7,6},{8,9},{9,8},{10,11... | collective-permute-start | bytes 1179656 | tf_op jit(solution)/shard_map/ppermute | solution.py:472
